TPU v7x, 32 devices: a whole 2x2x4 slice. The times are simulated.
32 devices in a mesh: ens: 2 (over y), gx: 4 (over x, core), gy: 4 (over z).
Axes of the slice: x: 2, y: 2, z: 4, core: 2. Of those that a mesh axis runs over, the one named last changes fastest.
Arguments:
- log_conductivity: float32 [64, 64, 256], P(('ens', 'gx'), 'gy'), parts along dimension 0, may hold values from -3 to 3
- state: float32 [64, 64, 256], P(('ens', 'gx'), 'gy'), parts along dimension 0, may hold values from -6 to 6
- gradient: float32 [64, 64, 256], P(('ens', 'gx'), 'gy'), parts along dimension 0, may hold values from -60 to 60
- prior_sample: float32 [64, 64, 256], P(('ens', 'gx'), 'gy'), parts along dimension 0, may hold values from -6 to 6
- sensor_cells: int32 [16384], P(('ens', 'gx', 'gy')), parts along dimension 0, may hold values from 0 to 524287, as said below
- noise_precision: float32 [16384], P(('ens', 'gx', 'gy')), parts along dimension 0, may hold values from 20 to 200
Outputs:
- step_field: float32 [64, 64, 256], P(('ens', 'gx'), 'gy'), parts along dimension 0
- residual: float32 [64, 64, 256], P(('ens', 'gx'), 'gy'), parts along dimension 0
There are 2 independent parts, one for each index of `ens`. A program takes and returns all parts, laid end to end along the dimension named above; each array names one. Nothing has to cross between parts.
Inputs may be any that keep to these rules, and one draw needn't show every extreme that they name: `sensor_cells`: sensors t * 512 to (t + 1) * 512 - 1 observe cells inside the block of cells held by the t-th device in the order gx, then gy (blocks of 8 x 16 x 256 cells); a cell may be observed by several sensors.
All inputs are finite; a program needn't handle non-finite values.
Results may differ from a plain program's by a relative error of at most 0.00015.
Values sent between devices are 32-bit elements; how exact they have to be, the bound alone decides.
No kernel may reach another device: no remote copies, remote signals or barrier semaphores. Data moves between devices by JAX's collectives and lax.ppermute only.
A program may use at most 128 MiB of HBM per device.

v0:
```python
import jax
import jax.numpy as jnp
from jax import lax
from jax.sharding import PartitionSpec as P

LEVELS = 3
SWEEPS = 1
COARSE_SWEEPS = 6
CG_ITERS = 2
DAMPING = 0.8
PRIOR_MASS = 0.5
PRIOR_STIFF = 1.0


def extended(x, sides, width):
    for axis, dim in sides:
        peers, length = (lax.axis_size(axis), x.shape[dim])
        up = [(i, (i + 1) % peers) for i in range(peers - 1)]
        down = [(j, i) for i, j in up]
        last = lax.slice_in_dim(x, length - width, length, axis=dim)
        leading = lax.slice_in_dim(x, 0, width, axis=dim)
        before = lax.ppermute(last, axis, up)
        after = lax.ppermute(leading, axis, down)
        x = jnp.concatenate([before, x, after], axis=dim)
    return x


def coarsen_sum(values):
    extent_x, extent_y, extent_z = values.shape
    blocks = values.reshape(extent_x // 2, 2, extent_y // 2, 2, extent_z // 2, 2)
    return blocks.sum(axis=(1, 3, 5))


def refine(values):
    return jnp.repeat(jnp.repeat(jnp.repeat(values, 2, axis=0), 2, axis=1), 2, axis=2)


def neighbours(padded):
    centre = padded[1:-1, 1:-1, :]
    border = jnp.zeros_like(centre[:, :, :1])
    beside = (
        padded[:-2, 1:-1, :],
        padded[2:, 1:-1, :],
        padded[1:-1, :-2, :],
        padded[1:-1, 2:, :],
        jnp.concatenate([border, centre[:, :, :-1]], axis=2),
        jnp.concatenate([centre[:, :, 1:], border], axis=2),
    )
    return (beside, centre)


def summed(entries):
    result = entries[0]
    for entry in entries[1:]:
        result = result + entry
    return result


def inside_flags(index_x, index_y, extent_x, extent_y, extent_z):
    index_z = jnp.arange(extent_z, dtype=jnp.int32)[None, None, :]
    return (
        index_x > 0,
        index_x < extent_x - 1,
        index_y > 0,
        index_y < extent_y - 1,
        index_z > 0,
        index_z < extent_z - 1,
    )


def face_weights(cond_padded, level_scale, interior):
    beside, centre = neighbours(cond_padded)
    return tuple(
        (
            level_scale * jnp.where(is_inner, 0.5 * (centre + neighbour), centre)
            for is_inner, neighbour in zip(interior, beside)
        )
    )


def apply_operator(padded, couplings, diagonal):
    beside, centre = neighbours(padded)
    return diagonal * centre - summed(
        [weight * neighbour for weight, neighbour in zip(couplings, beside)]
    )


def prior_apply(padded):
    beside, centre = neighbours(padded)
    return PRIOR_MASS * centre + PRIOR_STIFF * (6.0 * centre - summed(list(beside)))


def sensitivity(cond_padded, state_padded, probe_padded, interior):
    cond_side, cond_mid = neighbours(cond_padded)
    state_side, state_mid = neighbours(state_padded)
    probe_side, probe_mid = neighbours(probe_padded)
    flux_mid = cond_mid * probe_mid
    return summed(
        [
            jnp.where(is_inner, 0.5 * (flux_mid + cond_near * probe_near), flux_mid)
            * (state_mid - state_near)
            for is_inner, cond_near, probe_near, state_near in zip(
                interior, cond_side, probe_side, state_side
            )
        ]
    )


def misfit_gradient(cond_padded, state_padded, adjoint_padded, interior):
    cond_mid = neighbours(cond_padded)[1]
    state_side, state_mid = neighbours(state_padded)
    adjoint_side, adjoint_mid = neighbours(adjoint_padded)
    return cond_mid * summed(
        [
            jnp.where(is_inner, 0.5, 1.0) * (state_mid - state_near) * (adjoint_mid - adjoint_near)
            for is_inner, state_near, adjoint_near in zip(interior, state_side, adjoint_side)
        ]
    )


def smooth(iterate, source, couplings, diagonal, padder, sweeps):
    for sweep_index in range(sweeps):
        if iterate is None:
            iterate = DAMPING * source / diagonal
        else:
            iterate = (
                iterate
                + DAMPING
                * (source - apply_operator(padder(iterate), couplings, diagonal))
                / diagonal
            )
    return iterate


def vcycle(source, depth_index, operators, padders, coarse_solve):
    if depth_index == len(operators):
        return coarse_solve(source)
    couplings, diagonal = operators[depth_index]
    iterate = smooth(None, source, couplings, diagonal, padders[depth_index], SWEEPS)
    defect = source - apply_operator(padders[depth_index](iterate), couplings, diagonal)
    iterate = iterate + refine(
        vcycle(coarsen_sum(defect), depth_index + 1, operators, padders, coarse_solve)
    )
    return smooth(iterate, source, couplings, diagonal, padders[depth_index], SWEEPS)


def solve(source, operators, padders, coarse_solve):
    iterate = None
    iterate = vcycle(source, 0, operators, padders, coarse_solve)
    return iterate


def plain_pad(values):
    return jnp.pad(values, ((1, 1), (1, 1), (0, 0)))


def assemble(stacked, devices_x):
    pieces, extent_x, extent_y, extent_z = stacked.shape
    arranged = stacked.reshape(devices_x, pieces // devices_x, extent_x, extent_y, extent_z)
    return arranged.transpose(0, 2, 1, 3, 4).reshape(
        devices_x * extent_x, pieces // devices_x * extent_y, extent_z
    )


def norm_sum(residual):
    return lax.psum(jnp.sum(residual * residual), ("gx", "gy"))


def on_device(log_conductivity, state, gradient, prior_sample, sensor_cells, noise_precision):
    devices_x = lax.axis_size("gx")
    devices_y = lax.axis_size("gy")
    place_x = lax.axis_index("gx")
    place_y = lax.axis_index("gy")
    cells_x, cells_y, cells_z = log_conductivity.shape

    def fine_pad(values):
        return extended(values, (("gx", 0), ("gy", 1)), 1)

    def inner_pad(values):
        return extended(values, (("gx", 0), ("gy", 1)), 1)

    def local_flags(depth_index):
        factor = 2**depth_index
        extent_x = cells_x // factor
        extent_y = cells_y // factor
        index_x = place_x * extent_x + jnp.arange(extent_x, dtype=jnp.int32)[:, None, None]
        index_y = place_y * extent_y + jnp.arange(extent_y, dtype=jnp.int32)[None, :, None]
        return inside_flags(
            index_x, index_y, extent_x * devices_x, extent_y * devices_y, cells_z // factor
        )

    cond_levels = [jnp.exp(log_conductivity)]
    for depth_index in range(LEVELS - 1):
        cond_levels.append(coarsen_sum(cond_levels[-1]) / 8.0)
    padders = [fine_pad] + [inner_pad] * (LEVELS - 2)
    operators = []
    cond_padded = None
    for depth_index in range(LEVELS - 1):
        level_padded = padders[depth_index](cond_levels[depth_index])
        if depth_index == 0:
            cond_padded = level_padded
        couplings = face_weights(level_padded, float(2**depth_index), local_flags(depth_index))
        operators.append((couplings, summed(list(couplings))))
    coarsest = LEVELS - 1
    extent_x, extent_y, extent_z = cond_levels[coarsest].shape
    cond_whole = assemble(
        lax.all_gather(cond_levels[coarsest][None], ("gx", "gy"), axis=0, tiled=True), devices_x
    )
    whole_flags = inside_flags(
        jnp.arange(extent_x * devices_x, dtype=jnp.int32)[:, None, None],
        jnp.arange(extent_y * devices_y, dtype=jnp.int32)[None, :, None],
        extent_x * devices_x,
        extent_y * devices_y,
        extent_z,
    )
    coarse_couplings = face_weights(plain_pad(cond_whole), float(2**coarsest), whole_flags)
    coarse_diagonal = summed(list(coarse_couplings))

    def coarse_solve(source):
        gathered = assemble(
            lax.all_gather(source[None], ("gx", "gy"), axis=0, tiled=True), devices_x
        )
        answer = smooth(None, gathered, coarse_couplings, coarse_diagonal, plain_pad, COARSE_SWEEPS)
        return lax.dynamic_slice(
            answer,
            (place_x * extent_x, place_y * extent_y, place_x * 0),
            (extent_x, extent_y, extent_z),
        )

    fine_flags = local_flags(0)
    rows_all = cells_y * devices_y
    sensor_row = sensor_cells // (rows_all * cells_z)
    sensor_column = sensor_cells // cells_z % rows_all
    sensor_depth = sensor_cells % cells_z
    local_cell = (
        (sensor_row - place_x * cells_x) * cells_y + (sensor_column - place_y * cells_y)
    ) * cells_z + sensor_depth
    weight_field = (
        jnp.zeros((cells_x * cells_y * cells_z,), jnp.float32).at[local_cell].add(noise_precision)
    )
    weight_field = weight_field.reshape(cells_x, cells_y, cells_z)
    state_padded = fine_pad(state)
    source = prior_apply(fine_pad(prior_sample)) - gradient
    step_field = jnp.zeros_like(source)
    residual = source
    direction = residual
    norm_now = norm_sum(residual)
    for iteration in range(CG_ITERS):
        direction_padded = fine_pad(direction)
        change = solve(
            sensitivity(cond_padded, state_padded, direction_padded, fine_flags),
            operators,
            padders,
            coarse_solve,
        )
        adjoint = solve(weight_field * change, operators, padders, coarse_solve)
        curved = misfit_gradient(
            cond_padded, state_padded, fine_pad(adjoint), fine_flags
        ) + prior_apply(direction_padded)
        step_length = norm_now / lax.psum(jnp.sum(direction * curved), ("gx", "gy"))
        step_field = step_field + step_length * direction
        residual = residual - step_length * curved
        if iteration + 1 < CG_ITERS:
            norm_next = norm_sum(residual)
            direction = residual + norm_next / norm_now * direction
            norm_now = norm_next
    return (step_field, residual)


def solution(mesh):
    placed = (
        P(("ens", "gx"), "gy", None),
        P(("ens", "gx"), "gy", None),
        P(("ens", "gx"), "gy", None),
        P(("ens", "gx"), "gy", None),
        P(("ens", "gx", "gy")),
        P(("ens", "gx", "gy")),
    )
    return jax.shard_map(
        on_device,
        mesh=mesh,
        in_specs=placed,
        out_specs=(P(("ens", "gx"), "gy", None), P(("ens", "gx"), "gy", None)),
        check_vma=False,
    )
```

profile of v0, /device:TPU:10, one launch (start us, length us, event | category | flops | bytes accessed | tf_op | source)
XLA Modules:
  0.0 712.5 jit_solution(8180663991162468907)
XLA Ops:
  3.3 3.6 collective-permute-start.1
  9.8 3.6 collective-permute-start.7
  18.4 9.7 %reshape.259 = f32[4,2,8,2,128,2]{5,4,3,2,1,0:T(8,128)} reshape(f32[8,16,256]{2,1,0:T(8,128)S(1)} %exp.3) | data formatting | bytes 262144 | tf_op jit(solution)/shard_map/reshape | solution.py:30
  28.1 4.1 reduce_sum.128
  37.5 30.1 %all-gather.1 = f32[32,4,64]{2,1,0:T(4,128)S(1)} all-gather(f32[2,4,64]{2,1,0:T(4,128)S(1)} %broadcast_multiply_fusion.1), channel_id=3, replica_groups=mesh['ens'=2,'gx'=4,'gy'=4] {'gx','gy'}, dimensions={0}, use_global_device_ids=true | all-gather | bytes 34816 | tf_op jit(solution)/shard_map/all_gather | solution.py:207
  69.7 4.1 collective-permute-start.2
  73.9 3.2 collective-permute-start.3
  79.8 3.2 collective-permute-start.13
  85.1 3.6 collective-permute-start.8
  91.5 3.2 collective-permute-start.15
  97.4 3.1 collective-permute-start.14
  102.7 3.6 collective-permute-start.21
  108.9 3.6 collective-permute-start.17
  127.1 9.7 %reshape.258 = f32[4,2,8,2,128,2]{5,4,3,2,1,0:T(8,128)} reshape(f32[8,16,256]{2,1,0:T(8,128)S(1)} %fusion.126) | data formatting | bytes 262144 | tf_op jit(solution)/shard_map/reshape | solution.py:30
  136.9 4.0 reduce_sum.127
  143.1 3.6 collective-permute-start.25
  157.7 30.2 %all-gather = f32[32,4,64]{2,1,0:T(4,128)S(1)} all-gather(f32[2,4,64]{2,1,0:T(4,128)S(1)} %reduce_sum.129), channel_id=2, replica_groups=mesh['ens'=2,'gx'=4,'gy'=4] {'gx','gy'}, dimensions={0}, use_global_device_ids=true | all-gather | bytes 34816 | tf_op jit(solution)/shard_map/all_gather | solution.py:221
  192.0 3.6 collective-permute-start.29
  198.9 3.9 collective-permute-start.31
  209.0 3.8 collective-permute-start.33
  213.5 3.5 scatter_custom_fusion
  219.1 3.8 collective-permute-start.35
  227.5 3.6 collective-permute-start.37
  234.5 3.9 collective-permute-start.39
  240.9 9.7 %reshape.271 = f32[4,2,8,2,128,2]{5,4,3,2,1,0:T(8,128)} reshape(f32[8,16,256]{2,1,0:T(8,128)S(1)} %fusion.100) | data formatting | bytes 262144 | tf_op jit(solution)/shard_map/reshape | solution.py:30
  250.6 4.0 reduce_sum.131
  256.6 3.6 collective-permute-start.41
  263.5 3.9 collective-permute-start.43
  270.3 31.1 %all-gather.2 = f32[32,4,64]{2,1,0:T(4,128)S(1)} all-gather(f32[2,4,64]{2,1,0:T(4,128)S(1)} %reduce_sum.132), channel_id=4, replica_groups=mesh['ens'=2,'gx'=4,'gy'=4] {'gx','gy'}, dimensions={0}, use_global_device_ids=true | all-gather | bytes 34816 | tf_op jit(solution)/shard_map/all_gather | solution.py:221
  305.4 3.6 collective-permute-start.45
  312.3 3.9 collective-permute-start.47
  322.4 3.6 collective-permute-start.49
  329.6 3.8 collective-permute-start.51
  337.9 3.6 collective-permute-start.53
  344.9 3.9 collective-permute-start.55
  352.5 32.5 %all-reduce.111 = (f32[]{:T(128)}, f32[]{:T(128)}) all-reduce(f32[]{:T(128)} %get-tuple-element.5, f32[]{:T(128)} %get-tuple-element.4), channel_id=1, replica_groups=mesh['ens'=2,'gx'=4,'gy'=4] {'gx','gy'}, use_global_device_ids=true, to_apply=%region_1.0 | all-reduce | flops 2 | bytes 16 | tf_op jit(solution)/shard_map/psum | solution.py:166
  387.0 30.4 %psum.30 = f32[]{:T(128)} all-reduce(f32[]{:T(128)} %multiply_reduce_fusion.1), channel_id=1, replica_groups=mesh['ens'=2,'gx'=4,'gy'=4] {'gx','gy'}, use_global_device_ids=true, to_apply=%region_12.13 | all-reduce | flops 1 | bytes 8 | tf_op jit(solution)/shard_map/psum | solution.py:166
  420.7 3.6 collective-permute-start.57
  427.8 3.9 collective-permute-start.59
  436.7 3.6 collective-permute-start.61
  443.8 3.9 collective-permute-start.63
  450.2 9.7 %reshape.281 = f32[4,2,8,2,128,2]{5,4,3,2,1,0:T(8,128)} reshape(f32[8,16,256]{2,1,0:T(8,128)S(1)} %fusion.60) | data formatting | bytes 262144 | tf_op jit(solution)/shard_map/reshape | solution.py:30
  459.9 4.0 reduce_sum.135
  465.9 3.9 collective-permute-start.65
  472.8 3.9 collective-permute-start.67
  479.5 31.1 %all-gather.3 = f32[32,4,64]{2,1,0:T(4,128)S(1)} all-gather(f32[2,4,64]{2,1,0:T(4,128)S(1)} %reduce_sum.136), channel_id=5, replica_groups=mesh['ens'=2,'gx'=4,'gy'=4] {'gx','gy'}, dimensions={0}, use_global_device_ids=true | all-gather | bytes 34816 | tf_op jit(solution)/shard_map/all_gather | solution.py:221
  514.7 3.6 collective-permute-start.69
  521.6 3.9 collective-permute-start.71
  531.7 3.6 collective-permute-start.73
  538.9 3.8 collective-permute-start.75
  547.5 3.6 collective-permute-start.77
  554.5 3.9 collective-permute-start.79
  560.9 9.7 %reshape.291 = f32[4,2,8,2,128,2]{5,4,3,2,1,0:T(8,128)} reshape(f32[8,16,256]{2,1,0:T(8,128)S(1)} %fusion.34) | data formatting | bytes 262144 | tf_op jit(solution)/shard_map/reshape | solution.py:30
  570.6 4.0 reduce_sum.137
  576.7 3.6 collective-permute-start.81
  583.6 3.9 collective-permute-start.83
  592.3 31.5 %all-gather.4 = f32[32,4,64]{2,1,0:T(4,128)S(1)} all-gather(f32[2,4,64]{2,1,0:T(4,128)} %reduce_sum.138), channel_id=6, replica_groups=mesh['ens'=2,'gx'=4,'gy'=4] {'gx','gy'}, dimensions={0}, use_global_device_ids=true | all-gather | bytes 34816 | tf_op jit(solution)/shard_map/all_gather | solution.py:221
  628.7 3.6 collective-permute-start.85
  635.6 3.9 collective-permute-start.87
  648.0 3.6 collective-permute-start.89
  655.1 3.8 collective-permute-start.91
  663.5 3.6 collective-permute-start.93
  670.5 3.9 collective-permute-start.95
  677.9 32.5 %psum.31 = f32[]{:T(128)} all-reduce(f32[]{:T(128)} %get-tuple-element.8), channel_id=1, replica_groups=mesh['ens'=2,'gx'=4,'gy'=4] {'gx','gy'}, use_global_device_ids=true, to_apply=%region_18.19 | all-reduce | flops 1 | bytes 8 | tf_op jit(solution)/shard_map/psum | solution.py:260
  (530 shorter events, 216.1 us)
Async XLA Ops:
  1.4 66.3 %collective-permute-start = (f32[1,16,256]{2,1,0:T(8,128)S(1)}, f32[1,16,256]{2,1,0:T(8,128)S(1)}, u32[]{:S(2)}, u32[]{:S(2)}) collective-permute-start(f32[1,16,256]{2,1,0:T(8,128)S(1)} %get-tuple-element.130), channel_id=1, source_target_pairs={{0,4},{4,8},{8,12},{1,5},{5,9},{9,13},{2,6},{6,10},{10,14},{3,7},{... | collective-permute-start | bytes 49160 | tf_op jit(solution)/shard_map/ppermute | solution.py:22
  3.3 66.4 %collective-permute-start.1 = (f32[1,16,256]{2,1,0:T(8,128)S(1)}, f32[1,16,256]{2,1,0:T(8,128)S(1)}, u32[]{:S(2)}, u32[]{:S(2)}) collective-permute-start(f32[1,16,256]{2,1,0:T(8,128)S(1)} %get-tuple-element.129), channel_id=1, source_target_pairs={{4,0},{8,4},{12,8},{5,1},{9,5},{13,9},{6,2},{10,6},{14,10},{7,3},{... | collective-permute-start | bytes 49160 | tf_op jit(solution)/shard_map/ppermute | solution.py:23
  7.9 66.0 %collective-permute-start.5 = (f32[1,16,256]{2,1,0:T(8,128)S(1)}, f32[1,16,256]{2,1,0:T(8,128)S(1)}, u32[]{:S(2)}, u32[]{:S(2)}) collective-permute-start(f32[1,16,256]{2,1,0:T(8,128)S(1)} %get-tuple-element.121), channel_id=1, source_target_pairs={{0,4},{4,8},{8,12},{1,5},{5,9},{9,13},{2,6},{6,10},{10,14},{3,7},{... | collective-permute-start | bytes 49160 | tf_op jit(solution)/shard_map/ppermute | solution.py:22
  9.8 67.3 %collective-permute-start.7 = (f32[1,16,256]{2,1,0:T(8,128)S(1)}, f32[1,16,256]{2,1,0:T(8,128)S(1)}, u32[]{:S(2)}, u32[]{:S(2)}) collective-permute-start(f32[1,16,256]{2,1,0:T(8,128)S(1)} %get-tuple-element.122), channel_id=1, source_target_pairs={{4,0},{8,4},{12,8},{5,1},{9,5},{13,9},{6,2},{10,6},{14,10},{7,3},{... | collective-permute-start | bytes 49160 | tf_op jit(solution)/shard_map/ppermute | solution.py:23
  14.2 65.6 %collective-permute-start.4 = (f32[1,16,256]{2,1,0:T(8,128)S(1)}, f32[1,16,256]{2,1,0:T(8,128)S(1)}, u32[]{:S(2)}, u32[]{:S(2)}) collective-permute-start(f32[1,16,256]{2,1,0:T(8,128)S(1)} %get-tuple-element.116), channel_id=1, source_target_pairs={{0,4},{4,8},{8,12},{1,5},{5,9},{9,13},{2,6},{6,10},{10,14},{3,7},{... | collective-permute-start | bytes 49160 | tf_op jit(solution)/shard_map/ppermute | solution.py:22
  67.7 15.3 %collective-permute-start.9 = (f32[1,16,256]{2,1,0:T(8,128)S(1)}, f32[1,16,256]{2,1,0:T(8,128)S(1)}, u32[]{:S(2)}, u32[]{:S(2)}) collective-permute-start(f32[1,16,256]{2,1,0:T(8,128)S(1)} %get-tuple-element.115), channel_id=1, source_target_pairs={{4,0},{8,4},{12,8},{5,1},{9,5},{13,9},{6,2},{10,6},{14,10},{7,3},{... | collective-permute-start | bytes 49160 | tf_op jit(solution)/shard_map/ppermute | solution.py:23
  69.7 13.3 %collective-permute-start.2 = (f32[10,1,256]{2,1,0:T(1,128)S(1)}, f32[10,1,256]{2,1,0:T(1,128)S(1)}, u32[]{:S(2)}, u32[]{:S(2)}) collective-permute-start(f32[10,1,256]{2,1,0:T(1,128)S(1)} %get-tuple-element.67), channel_id=1, source_target_pairs={{0,1},{1,2},{2,3},{4,5},{5,6},{6,7},{8,9},{9,10},{10,11},{12,13},{... | collective-permute-start | bytes 30728 | tf_op jit(solution)/shard_map/ppermute | solution.py:22
  73.9 9.2 %collective-permute-start.3 = (f32[10,1,256]{2,1,0:T(1,128)S(1)}, f32[10,1,256]{2,1,0:T(1,128)S(1)}, u32[]{:S(2)}, u32[]{:S(2)}) collective-permute-start(f32[10,1,256]{2,1,0:T(1,128)S(1)} %get-tuple-element.68), channel_id=1, source_target_pairs={{1,0},{2,1},{3,2},{5,4},{6,5},{7,6},{9,8},{10,9},{11,10},{13,12},{... | collective-permute-start | bytes 30728 | tf_op jit(solution)/shard_map/ppermute | solution.py:23
  77.1 20.3 %collective-permute-start.10 = (f32[10,1,256]{2,1,0:T(1,128)S(1)}, f32[10,1,256]{2,1,0:T(1,128)S(1)}, u32[]{:S(2)}, u32[]{:S(2)}) collective-permute-start(f32[10,1,256]{2,1,0:T(1,128)S(1)} %get-tuple-element.64), channel_id=1, source_target_pairs={{0,1},{1,2},{2,3},{4,5},{5,6},{6,7},{8,9},{9,10},{10,11},{12,13},{... | collective-permute-start | bytes 30728 | tf_op jit(solution)/shard_map/ppermute | solution.py:22
  79.8 20.9 %collective-permute-start.13 = (f32[10,1,256]{2,1,0:T(1,128)S(1)}, f32[10,1,256]{2,1,0:T(1,128)S(1)}, u32[]{:S(2)}, u32[]{:S(2)}) collective-permute-start(f32[10,1,256]{2,1,0:T(1,128)S(1)} %get-tuple-element.63), channel_id=1, source_target_pairs={{1,0},{2,1},{3,2},{5,4},{6,5},{7,6},{9,8},{10,9},{11,10},{13,12},{... | collective-permute-start | bytes 30728 | tf_op jit(solution)/shard_map/ppermute | solution.py:23
  83.2 8.3 %collective-permute-start.6 = (f32[1,16,256]{2,1,0:T(8,128)S(1)}, f32[1,16,256]{2,1,0:T(8,128)S(1)}, u32[]{:S(2)}, u32[]{:S(2)}) collective-permute-start(f32[1,16,256]{2,1,0:T(8,128)S(1)} %get-tuple-element.123), channel_id=1, source_target_pairs={{0,4},{4,8},{8,12},{1,5},{5,9},{9,13},{2,6},{6,10},{10,14},{3,7},{... | collective-permute-start | bytes 49160 | tf_op jit(solution)/shard_map/ppermute | solution.py:22
  85.1 9.6 %collective-permute-start.8 = (f32[1,16,256]{2,1,0:T(8,128)S(1)}, f32[1,16,256]{2,1,0:T(8,128)S(1)}, u32[]{:S(2)}, u32[]{:S(2)}) collective-permute-start(f32[1,16,256]{2,1,0:T(8,128)S(1)} %get-tuple-element.124), channel_id=1, source_target_pairs={{4,0},{8,4},{12,8},{5,1},{9,5},{13,9},{6,2},{10,6},{14,10},{7,3},{... | collective-permute-start | bytes 49160 | tf_op jit(solution)/shard_map/ppermute | solution.py:23
  88.8 13.9 %collective-permute-start.12 = (f32[10,1,256]{2,1,0:T(1,128)S(1)}, f32[10,1,256]{2,1,0:T(1,128)S(1)}, u32[]{:S(2)}, u32[]{:S(2)}) collective-permute-start(f32[10,1,256]{2,1,0:T(1,128)S(1)} %get-tuple-element.61), channel_id=1, source_target_pairs={{0,1},{1,2},{2,3},{4,5},{5,6},{6,7},{8,9},{9,10},{10,11},{12,13},{... | collective-permute-start | bytes 30728 | tf_op jit(solution)/shard_map/ppermute | solution.py:22
  91.5 14.8 %collective-permute-start.15 = (f32[10,1,256]{2,1,0:T(1,128)S(1)}, f32[10,1,256]{2,1,0:T(1,128)S(1)}, u32[]{:S(2)}, u32[]{:S(2)}) collective-permute-start(f32[10,1,256]{2,1,0:T(1,128)S(1)} %get-tuple-element.62), channel_id=1, source_target_pairs={{1,0},{2,1},{3,2},{5,4},{6,5},{7,6},{9,8},{10,9},{11,10},{13,12},{... | collective-permute-start | bytes 30728 | tf_op jit(solution)/shard_map/ppermute | solution.py:23
  94.7 11.6 %collective-permute-start.11 = (f32[10,1,256]{2,1,0:T(1,128)S(1)}, f32[10,1,256]{2,1,0:T(1,128)S(1)}, u32[]{:S(2)}, u32[]{:S(2)}) collective-permute-start(f32[10,1,256]{2,1,0:T(1,128)S(1)} %get-tuple-element.65), channel_id=1, source_target_pairs={{0,1},{1,2},{2,3},{4,5},{5,6},{6,7},{8,9},{9,10},{10,11},{12,13},{... | collective-permute-start | bytes 30728 | tf_op jit(solution)/shard_map/ppermute | solution.py:22
  97.4 8.9 %collective-permute-start.14 = (f32[10,1,256]{2,1,0:T(1,128)S(1)}, f32[10,1,256]{2,1,0:T(1,128)S(1)}, u32[]{:S(2)}, u32[]{:S(2)}) collective-permute-start(f32[10,1,256]{2,1,0:T(1,128)S(1)} %get-tuple-element.66), channel_id=1, source_target_pairs={{1,0},{2,1},{3,2},{5,4},{6,5},{7,6},{9,8},{10,9},{11,10},{13,12},{... | collective-permute-start | bytes 30728 | tf_op jit(solution)/shard_map/ppermute | solution.py:23
  100.7 11.8 %collective-permute-start.20 = (f32[1,8,128]{2,1,0:T(8,128)S(1)}, f32[1,8,128]{2,1,0:T(8,128)S(1)}, u32[]{:S(2)}, u32[]{:S(2)}) collective-permute-start(f32[1,8,128]{2,1,0:T(8,128)S(1)} %get-tuple-element.225), channel_id=1, source_target_pairs={{0,4},{4,8},{8,12},{1,5},{5,9},{9,13},{2,6},{6,10},{10,14},{3,7},{... | collective-permute-start | bytes 12296 | tf_op jit(solution)/shard_map/ppermute | solution.py:22
  102.7 9.9 %collective-permute-start.21 = (f32[1,8,128]{2,1,0:T(8,128)S(1)}, f32[1,8,128]{2,1,0:T(8,128)S(1)}, u32[]{:S(2)}, u32[]{:S(2)}) collective-permute-start(f32[1,8,128]{2,1,0:T(8,128)S(1)} %get-tuple-element.226), channel_id=1, source_target_pairs={{4,0},{8,4},{12,8},{5,1},{9,5},{13,9},{6,2},{10,6},{14,10},{7,3},{... | collective-permute-start | bytes 12296 | tf_op jit(solution)/shard_map/ppermute | solution.py:23
  107.0 11.5 %collective-permute-start.16 = (f32[1,16,256]{2,1,0:T(8,128)S(1)}, f32[1,16,256]{2,1,0:T(8,128)S(1)}, u32[]{:S(2)}, u32[]{:S(2)}) collective-permute-start(f32[1,16,256]{2,1,0:T(8,128)S(1)} %get-tuple-element.113), channel_id=1, source_target_pairs={{0,4},{4,8},{8,12},{1,5},{5,9},{9,13},{2,6},{6,10},{10,14},{3,7},{... | collective-permute-start | bytes 49160 | tf_op jit(solution)/shard_map/ppermute | solution.py:22
  108.9 9.6 %collective-permute-start.17 = (f32[1,16,256]{2,1,0:T(8,128)S(1)}, f32[1,16,256]{2,1,0:T(8,128)S(1)}, u32[]{:S(2)}, u32[]{:S(2)}) collective-permute-start(f32[1,16,256]{2,1,0:T(8,128)S(1)} %get-tuple-element.114), channel_id=1, source_target_pairs={{4,0},{8,4},{12,8},{5,1},{9,5},{13,9},{6,2},{10,6},{14,10},{7,3},{... | collective-permute-start | bytes 49160 | tf_op jit(solution)/shard_map/ppermute | solution.py:23
  112.6 28.4 %collective-permute-start.22 = (f32[6,1,128]{2,1,0:T(1,128)S(1)}, f32[6,1,128]{2,1,0:T(1,128)S(1)}, u32[]{:S(2)}, u32[]{:S(2)}) collective-permute-start(f32[6,1,128]{2,1,0:T(1,128)S(1)} %get-tuple-element.190), channel_id=1, source_target_pairs={{0,1},{1,2},{2,3},{4,5},{5,6},{6,7},{8,9},{9,10},{10,11},{12,13},{... | collective-permute-start | bytes 9224 | tf_op jit(solution)/shard_map/ppermute | solution.py:22
  115.3 25.7 %collective-permute-start.23 = (f32[6,1,128]{2,1,0:T(1,128)S(1)}, f32[6,1,128]{2,1,0:T(1,128)S(1)}, u32[]{:S(2)}, u32[]{:S(2)}) collective-permute-start(f32[6,1,128]{2,1,0:T(1,128)S(1)} %get-tuple-element.189), channel_id=1, source_target_pairs={{1,0},{2,1},{3,2},{5,4},{6,5},{7,6},{9,8},{10,9},{11,10},{13,12},{... | collective-permute-start | bytes 9224 | tf_op jit(solution)/shard_map/ppermute | solution.py:23
  118.5 6.0 collective-permute-start.18
  121.2 5.6 collective-permute-start.19
  141.2 6.4 collective-permute-start.24
  148.1 5.9 collective-permute-start.26
  190.1 5.6 collective-permute-start.28
  196.9 5.9 collective-permute-start.30
  207.1 10.0 %collective-permute-start.32 = (f32[1,16,256]{2,1,0:T(8,128)S(1)}, f32[1,16,256]{2,1,0:T(8,128)S(1)}, u32[]{:S(2)}, u32[]{:S(2)}) collective-permute-start(f32[1,16,256]{2,1,0:T(8,128)S(1)} %get-tuple-element.107), channel_id=1, source_target_pairs={{0,4},{4,8},{8,12},{1,5},{5,9},{9,13},{2,6},{6,10},{10,14},{3,7},{... | collective-permute-start | bytes 49160 | tf_op jit(solution)/shard_map/ppermute | solution.py:22
  209.0 8.1 %collective-permute-start.33 = (f32[1,16,256]{2,1,0:T(8,128)S(1)}, f32[1,16,256]{2,1,0:T(8,128)S(1)}, u32[]{:S(2)}, u32[]{:S(2)}) collective-permute-start(f32[1,16,256]{2,1,0:T(8,128)S(1)} %get-tuple-element.108), channel_id=1, source_target_pairs={{4,0},{8,4},{12,8},{5,1},{9,5},{13,9},{6,2},{10,6},{14,10},{7,3},{... | collective-permute-start | bytes 49160 | tf_op jit(solution)/shard_map/ppermute | solution.py:23
  217.1 6.0 collective-permute-start.34
  219.1 5.6 collective-permute-start.35
  225.6 5.6 collective-permute-start.36
  232.6 6.0 collective-permute-start.38
  234.5 5.6 collective-permute-start.39
  254.7 5.6 collective-permute-start.40
  261.6 5.9 collective-permute-start.42
  303.5 6.2 collective-permute-start.44
  310.4 5.9 collective-permute-start.46
  320.5 5.6 collective-permute-start.48
  327.5 6.0 collective-permute-start.50
  336.0 5.6 collective-permute-start.52
  343.0 6.0 collective-permute-start.54
  418.8 5.6 collective-permute-start.56
  425.8 6.0 collective-permute-start.58
  434.8 5.6 collective-permute-start.60
  441.8 6.0 collective-permute-start.62
  464.0 5.8 collective-permute-start.64
  470.9 5.9 collective-permute-start.66
  512.8 5.6 collective-permute-start.68
  519.7 5.9 collective-permute-start.70
  529.8 5.6 collective-permute-start.72
  536.8 6.0 collective-permute-start.74
  545.6 5.6 collective-permute-start.76
  552.6 6.0 collective-permute-start.78
  574.7 5.7 collective-permute-start.80
  581.7 5.9 collective-permute-start.82
  626.8 5.6 collective-permute-start.84
  633.7 5.9 collective-permute-start.86
  646.1 5.6 collective-permute-start.88
  653.1 6.0 collective-permute-start.90
  661.5 5.6 collective-permute-start.92
  668.6 6.0 collective-permute-start.94
  670.5 5.6 collective-permute-start.95
  (99 other events, 3230.6 us)
where the time goes:
time: 717 us; the launch traced here: 712 us
  starting transfers between devices  274 us (38%)
  blocking collectives  250 us (35%)
  local copies, waits for them, and re-layouts  75.6 us (11%)
  other arithmetic  53.2 us (7%)
  waiting for transfers between devices  52.6 us (7%)
  between operations  7.76 us (1%)
    ppermute x48, starting transfers between devices, extended(): after = lax.ppermute(leading, axis, down)  174 us
    all_gather x4, blocking collectives, coarse_solve(): lax.all_gather(source[None], ('gx', 'gy'), axis=0, tiled=True)  124 us
    ppermute x48, starting transfers between devices, extended(): before = lax.ppermute(last, axis, up)  99.9 us
    psum x2, blocking collectives, norm_sum(): return lax.psum(jnp.sum(residual * residual), ('gx', 'gy'))  62.9 us
    reshape x9, local copies, waits for them, and re-layouts, coarsen_sum(): values.reshape(extent_x // 2, 2, extent_y // 2, 2, extent_z // 2, 2)  53.3 us
    ppermute x48, waiting for transfers between devices, extended(): after = lax.ppermute(leading, axis, down)  52.5 us
    psum x1, blocking collectives, on_device(): step_length = norm_now / lax.psum(jnp.sum(direction * curved), ('gx', 'gy'))  32.5 us
    all_gather x1, blocking collectives, on_device(): lax.all_gather(cond_levels[coarsest][None], ('gx', 'gy'), axis=0, tiled=T...  30.1 us
  transfers between devices with their start and end apart: 96, of which 36 were waited for; matrix products, arithmetic and copies ran while one was open for 6% of the time, Pallas kernels for 0%

commit v1 on v0

--- a/solution.py
+++ b/solution.py
@@ -10,6 +10,18 @@
 DAMPING = 0.8
 PRIOR_MASS = 0.5
 PRIOR_STIFF = 1.0
+
+
+def gather_around(value, axis, dim):
+    ways, here, step = (lax.axis_size(axis), lax.axis_index(axis), value.shape[dim])
+    shape = [n * ways if d == dim else n for d, n in enumerate(value.shape)]
+    full = lax.dynamic_update_slice_in_dim(
+        jnp.zeros(shape, value.dtype), value, here * step, axis=dim
+    )
+    for far in range(1, ways):
+        value = lax.ppermute(value, axis, [(d, (d + 1) % ways) for d in range(ways)])
+        full = lax.dynamic_update_slice_in_dim(full, value, (here - far) % ways * step, axis=dim)
+    return full
 
 
 def extended(x, sides, width):
@@ -217,9 +229,7 @@
     coarse_diagonal = summed(list(coarse_couplings))
 
     def coarse_solve(source):
-        gathered = assemble(
-            lax.all_gather(source[None], ("gx", "gy"), axis=0, tiled=True), devices_x
-        )
+        gathered = assemble(gather_around(source[None], ("gx", "gy"), 0), devices_x)
         answer = smooth(None, gathered, coarse_couplings, coarse_diagonal, plain_pad, COARSE_SWEEPS)
         return lax.dynamic_slice(
             answer,

time: 717 us -> 934 us (1.30)
  waiting for transfers between devices: 52.6 us -> 375 us
  blocking collectives: 250 us -> 129 us
    ppermute x0 -> x60, waiting for transfers between devices: none -> 319 us  [gather_around(): lax.ppermute(value, axis, [(d, (d + 1) % ways) for d in range(ways)])]
    all_gather x4 -> x0, blocking collectives: 124 us -> none  [coarse_solve(): lax.all_gather(source[None], ('gx', 'gy'), axis=0, tiled=True)]
  transfers between devices with their start and end apart: 96 -> 156, of which waited for: 36 -> 95; matrix products, arithmetic and copies ran while one was open for 6% -> 5% of each run, Pallas kernels for 0% -> 0%
where the time goes in v1:
time: 934 us; the launch traced here: 922 us
  waiting for transfers between devices  375 us (40%)
  starting transfers between devices  283 us (30%)
  blocking collectives  129 us (14%)
  local copies, waits for them, and re-layouts  79.3 us (8%)
  other arithmetic  47.9 us (5%)
    ppermute x60, waiting for transfers between devices, gather_around(): lax.ppermute(value, axis, [(d, (d + 1) % ways) for d in range(ways)])  319 us
    ppermute x48, starting transfers between devices, extended(): after = lax.ppermute(leading, axis, down)  174 us
    ppermute x48, starting transfers between devices, extended(): before = lax.ppermute(last, axis, up)  106 us
    psum x2, blocking collectives, norm_sum(): return lax.psum(jnp.sum(residual * residual), ('gx', 'gy'))  62.9 us
    ppermute x48, waiting for transfers between devices, extended(): after = lax.ppermute(leading, axis, down)  55.3 us
    reshape x9, local copies, waits for them, and re-layouts, coarsen_sum(): values.reshape(extent_x // 2, 2, extent_y // 2, 2, extent_z // 2, 2)  53.3 us
    all_gather x1, blocking collectives, on_device(): lax.all_gather(cond_levels[coarsest][None], ('gx', 'gy'), axis=0, tiled=T...  33.3 us
    psum x1, blocking collectives, on_device(): step_length = norm_now / lax.psum(jnp.sum(direction * curved), ('gx', 'gy'))  32.5 us
  transfers between devices with their start and end apart: 156, of which 95 were waited for; matrix products, arithmetic and copies ran while one was open for 5% of the time, Pallas kernels for 0%

profile of v1, /device:TPU:10, one launch (start us, length us, event | category | flops | bytes accessed | tf_op | source)
XLA Modules:
  0.0 921.7 jit_solution(14611074900826365713)
XLA Ops:
  18.4 9.7 %reshape.259 = f32[4,2,8,2,128,2]{5,4,3,2,1,0:T(8,128)} reshape(f32[8,16,256]{2,1,0:T(8,128)S(1)} %exp.3) | data formatting | bytes 262144 | tf_op jit(solution)/shard_map/reshape | solution.py:42
  92.8 9.7 %reshape.258 = f32[4,2,8,2,128,2]{5,4,3,2,1,0:T(8,128)} reshape(f32[8,16,256]{2,1,0:T(8,128)S(1)} %fusion.126) | data formatting | bytes 262144 | tf_op jit(solution)/shard_map/reshape | solution.py:42
  131.7 5.7 collective-permute-done.30
  137.4 33.3 %all-gather = f32[32,4,64]{2,1,0:T(4,128)S(1)} all-gather(f32[2,4,64]{2,1,0:T(4,128)S(1)} %broadcast_multiply_fusion.1), channel_id=2, replica_groups=mesh['ens'=2,'gx'=4,'gy'=4] {'gx','gy'}, dimensions={0}, use_global_device_ids=true | all-gather | bytes 34816 | tf_op jit(solution)/shard_map/all_gather | solution.py:219
  176.7 5.6 collective-permute-done.33
  182.3 5.7 collective-permute-done.34
  188.1 5.7 collective-permute-done.35
  193.9 5.6 collective-permute-done.36
  199.5 5.7 collective-permute-done.37
  205.2 5.7 collective-permute-done.38
  211.0 5.7 collective-permute-done.39
  216.7 5.7 collective-permute-done.40
  222.4 5.7 collective-permute-done.41
  244.6 5.4 collective-permute-start.46
  288.5 9.7 %reshape.271 = f32[4,2,8,2,128,2]{5,4,3,2,1,0:T(8,128)} reshape(f32[8,16,256]{2,1,0:T(8,128)S(1)} %fusion.100) | data formatting | bytes 262144 | tf_op jit(solution)/shard_map/reshape | solution.py:42
  321.6 5.7 collective-permute-done.60
  327.3 5.7 collective-permute-done.61
  333.0 5.7 collective-permute-done.62
  338.7 5.7 collective-permute-done.63
  344.5 5.7 collective-permute-done.64
  350.2 5.7 collective-permute-done.65
  355.9 5.7 collective-permute-done.66
  361.7 5.7 collective-permute-done.67
  367.4 5.7 collective-permute-done.68
  373.1 5.7 collective-permute-done.69
  378.9 5.7 collective-permute-done.70
  384.6 5.7 collective-permute-done.71
  390.3 5.7 collective-permute-done.72
  396.7 5.0 collective-permute-done.73
  412.7 5.4 collective-permute-start.77
  454.3 32.5 %all-reduce.111 = (f32[]{:T(128)}, f32[]{:T(128)}) all-reduce(f32[]{:T(128)} %get-tuple-element.5, f32[]{:T(128)} %get-tuple-element.4), channel_id=1, replica_groups=mesh['ens'=2,'gx'=4,'gy'=4] {'gx','gy'}, use_global_device_ids=true, to_apply=%region_1.0 | all-reduce | flops 2 | bytes 16 | tf_op jit(solution)/shard_map/psum | solution.py:178
  488.8 30.4 %psum.30 = f32[]{:T(128)} all-reduce(f32[]{:T(128)} %multiply_reduce_fusion.1), channel_id=1, replica_groups=mesh['ens'=2,'gx'=4,'gy'=4] {'gx','gy'}, use_global_device_ids=true, to_apply=%region_12.13 | all-reduce | flops 1 | bytes 8 | tf_op jit(solution)/shard_map/psum | solution.py:178
  551.9 9.7 %reshape.281 = f32[4,2,8,2,128,2]{5,4,3,2,1,0:T(8,128)} reshape(f32[8,16,256]{2,1,0:T(8,128)S(1)} %fusion.60) | data formatting | bytes 262144 | tf_op jit(solution)/shard_map/reshape | solution.py:42
  585.0 5.7 collective-permute-done.99
  590.7 5.7 collective-permute-done.100
  596.4 5.7 collective-permute-done.101
  602.1 5.7 collective-permute-done.102
  607.9 5.7 collective-permute-done.103
  613.6 5.7 collective-permute-done.104
  619.3 5.7 collective-permute-done.105
  625.1 5.7 collective-permute-done.106
  630.8 5.7 collective-permute-done.107
  636.5 5.7 collective-permute-done.108
  642.2 5.7 collective-permute-done.109
  648.0 5.7 collective-permute-done.110
  653.7 5.7 collective-permute-done.111
  660.1 5.0 collective-permute-done.112
  676.1 5.4 collective-permute-start.116
  716.8 9.7 %reshape.291 = f32[4,2,8,2,128,2]{5,4,3,2,1,0:T(8,128)} reshape(f32[8,16,256]{2,1,0:T(8,128)S(1)} %fusion.34) | data formatting | bytes 262144 | tf_op jit(solution)/shard_map/reshape | solution.py:42
  752.0 5.7 collective-permute-done.130
  757.7 5.7 collective-permute-done.131
  763.5 5.7 collective-permute-done.132
  769.2 5.7 collective-permute-done.133
  774.9 5.7 collective-permute-done.134
  780.7 5.7 collective-permute-done.135
  786.4 5.7 collective-permute-done.136
  792.1 5.7 collective-permute-done.137
  797.9 5.7 collective-permute-done.138
  803.6 5.7 collective-permute-done.139
  809.3 5.7 collective-permute-done.140
  815.0 5.7 collective-permute-done.141
  820.8 5.7 collective-permute-done.142
  843.9 5.4 collective-permute-start.147
  886.8 32.5 %psum.31 = f32[]{:T(128)} all-reduce(f32[]{:T(128)} %get-tuple-element.8), channel_id=1, replica_groups=mesh['ens'=2,'gx'=4,'gy'=4] {'gx','gy'}, use_global_device_ids=true, to_apply=%region_18.19 | all-reduce | flops 1 | bytes 8 | tf_op jit(solution)/shard_map/psum | solution.py:270
  (674 shorter events, 424.2 us)
Async XLA Ops:
  1.4 31.0 %collective-permute-start = (f32[1,16,256]{2,1,0:T(8,128)S(1)}, f32[1,16,256]{2,1,0:T(8,128)S(1)}, u32[]{:S(2)}, u32[]{:S(2)}) collective-permute-start(f32[1,16,256]{2,1,0:T(8,128)S(1)} %get-tuple-element.130), channel_id=1, source_target_pairs={{0,4},{4,8},{8,12},{1,5},{5,9},{9,13},{2,6},{6,10},{10,14},{3,7},{... | collective-permute-start | bytes 49160 | tf_op jit(solution)/shard_map/ppermute | solution.py:34
  3.3 32.8 %collective-permute-start.1 = (f32[1,16,256]{2,1,0:T(8,128)S(1)}, f32[1,16,256]{2,1,0:T(8,128)S(1)}, u32[]{:S(2)}, u32[]{:S(2)}) collective-permute-start(f32[1,16,256]{2,1,0:T(8,128)S(1)} %get-tuple-element.129), channel_id=1, source_target_pairs={{4,0},{8,4},{12,8},{5,1},{9,5},{13,9},{6,2},{10,6},{14,10},{7,3},{... | collective-permute-start | bytes 49160 | tf_op jit(solution)/shard_map/ppermute | solution.py:35
  7.9 31.7 %collective-permute-start.5 = (f32[1,16,256]{2,1,0:T(8,128)S(1)}, f32[1,16,256]{2,1,0:T(8,128)S(1)}, u32[]{:S(2)}, u32[]{:S(2)}) collective-permute-start(f32[1,16,256]{2,1,0:T(8,128)S(1)} %get-tuple-element.121), channel_id=1, source_target_pairs={{0,4},{4,8},{8,12},{1,5},{5,9},{9,13},{2,6},{6,10},{10,14},{3,7},{... | collective-permute-start | bytes 49160 | tf_op jit(solution)/shard_map/ppermute | solution.py:34
  9.8 32.2 %collective-permute-start.7 = (f32[1,16,256]{2,1,0:T(8,128)S(1)}, f32[1,16,256]{2,1,0:T(8,128)S(1)}, u32[]{:S(2)}, u32[]{:S(2)}) collective-permute-start(f32[1,16,256]{2,1,0:T(8,128)S(1)} %get-tuple-element.122), channel_id=1, source_target_pairs={{4,0},{8,4},{12,8},{5,1},{9,5},{13,9},{6,2},{10,6},{14,10},{7,3},{... | collective-permute-start | bytes 49160 | tf_op jit(solution)/shard_map/ppermute | solution.py:35
  14.2 31.3 %collective-permute-start.4 = (f32[1,16,256]{2,1,0:T(8,128)S(1)}, f32[1,16,256]{2,1,0:T(8,128)S(1)}, u32[]{:S(2)}, u32[]{:S(2)}) collective-permute-start(f32[1,16,256]{2,1,0:T(8,128)S(1)} %get-tuple-element.116), channel_id=1, source_target_pairs={{0,4},{4,8},{8,12},{1,5},{5,9},{9,13},{2,6},{6,10},{10,14},{3,7},{... | collective-permute-start | bytes 49160 | tf_op jit(solution)/shard_map/ppermute | solution.py:34
  32.4 15.6 %collective-permute-start.9 = (f32[1,16,256]{2,1,0:T(8,128)S(1)}, f32[1,16,256]{2,1,0:T(8,128)S(1)}, u32[]{:S(2)}, u32[]{:S(2)}) collective-permute-start(f32[1,16,256]{2,1,0:T(8,128)S(1)} %get-tuple-element.115), channel_id=1, source_target_pairs={{4,0},{8,4},{12,8},{5,1},{9,5},{13,9},{6,2},{10,6},{14,10},{7,3},{... | collective-permute-start | bytes 49160 | tf_op jit(solution)/shard_map/ppermute | solution.py:35
  36.1 11.9 %collective-permute-start.2 = (f32[10,1,256]{2,1,0:T(1,128)S(1)}, f32[10,1,256]{2,1,0:T(1,128)S(1)}, u32[]{:S(2)}, u32[]{:S(2)}) collective-permute-start(f32[10,1,256]{2,1,0:T(1,128)S(1)} %get-tuple-element.67), channel_id=1, source_target_pairs={{0,1},{1,2},{2,3},{4,5},{5,6},{6,7},{8,9},{9,10},{10,11},{12,13},{... | collective-permute-start | bytes 30728 | tf_op jit(solution)/shard_map/ppermute | solution.py:34
  39.6 8.4 collective-permute-start.3
  42.0 21.1 %collective-permute-start.10 = (f32[10,1,256]{2,1,0:T(1,128)S(1)}, f32[10,1,256]{2,1,0:T(1,128)S(1)}, u32[]{:S(2)}, u32[]{:S(2)}) collective-permute-start(f32[10,1,256]{2,1,0:T(1,128)S(1)} %get-tuple-element.64), channel_id=1, source_target_pairs={{0,1},{1,2},{2,3},{4,5},{5,6},{6,7},{8,9},{9,10},{10,11},{12,13},{... | collective-permute-start | bytes 30728 | tf_op jit(solution)/shard_map/ppermute | solution.py:34
  45.5 20.1 %collective-permute-start.13 = (f32[10,1,256]{2,1,0:T(1,128)S(1)}, f32[10,1,256]{2,1,0:T(1,128)S(1)}, u32[]{:S(2)}, u32[]{:S(2)}) collective-permute-start(f32[10,1,256]{2,1,0:T(1,128)S(1)} %get-tuple-element.63), channel_id=1, source_target_pairs={{1,0},{2,1},{3,2},{5,4},{6,5},{7,6},{9,8},{10,9},{11,10},{13,12},{... | collective-permute-start | bytes 30728 | tf_op jit(solution)/shard_map/ppermute | solution.py:35
  48.1 9.1 collective-permute-start.6
  50.1 9.6 %collective-permute-start.8 = (f32[1,16,256]{2,1,0:T(8,128)S(1)}, f32[1,16,256]{2,1,0:T(8,128)S(1)}, u32[]{:S(2)}, u32[]{:S(2)}) collective-permute-start(f32[1,16,256]{2,1,0:T(8,128)S(1)} %get-tuple-element.124), channel_id=1, source_target_pairs={{4,0},{8,4},{12,8},{5,1},{9,5},{13,9},{6,2},{10,6},{14,10},{7,3},{... | collective-permute-start | bytes 49160 | tf_op jit(solution)/shard_map/ppermute | solution.py:35
  53.7 13.9 %collective-permute-start.12 = (f32[10,1,256]{2,1,0:T(1,128)S(1)}, f32[10,1,256]{2,1,0:T(1,128)S(1)}, u32[]{:S(2)}, u32[]{:S(2)}) collective-permute-start(f32[10,1,256]{2,1,0:T(1,128)S(1)} %get-tuple-element.61), channel_id=1, source_target_pairs={{0,1},{1,2},{2,3},{4,5},{5,6},{6,7},{8,9},{9,10},{10,11},{12,13},{... | collective-permute-start | bytes 30728 | tf_op jit(solution)/shard_map/ppermute | solution.py:34
  57.3 14.0 %collective-permute-start.15 = (f32[10,1,256]{2,1,0:T(1,128)S(1)}, f32[10,1,256]{2,1,0:T(1,128)S(1)}, u32[]{:S(2)}, u32[]{:S(2)}) collective-permute-start(f32[10,1,256]{2,1,0:T(1,128)S(1)} %get-tuple-element.62), channel_id=1, source_target_pairs={{1,0},{2,1},{3,2},{5,4},{6,5},{7,6},{9,8},{10,9},{11,10},{13,12},{... | collective-permute-start | bytes 30728 | tf_op jit(solution)/shard_map/ppermute | solution.py:35
  59.7 11.6 %collective-permute-start.11 = (f32[10,1,256]{2,1,0:T(1,128)S(1)}, f32[10,1,256]{2,1,0:T(1,128)S(1)}, u32[]{:S(2)}, u32[]{:S(2)}) collective-permute-start(f32[10,1,256]{2,1,0:T(1,128)S(1)} %get-tuple-element.65), channel_id=1, source_target_pairs={{0,1},{1,2},{2,3},{4,5},{5,6},{6,7},{8,9},{9,10},{10,11},{12,13},{... | collective-permute-start | bytes 30728 | tf_op jit(solution)/shard_map/ppermute | solution.py:34
  63.2 8.1 collective-permute-start.14
  65.7 11.8 %collective-permute-start.20 = (f32[1,8,128]{2,1,0:T(8,128)S(1)}, f32[1,8,128]{2,1,0:T(8,128)S(1)}, u32[]{:S(2)}, u32[]{:S(2)}) collective-permute-start(f32[1,8,128]{2,1,0:T(8,128)S(1)} %get-tuple-element.225), channel_id=1, source_target_pairs={{0,4},{4,8},{8,12},{1,5},{5,9},{9,13},{2,6},{6,10},{10,14},{3,7},{... | collective-permute-start | bytes 12296 | tf_op jit(solution)/shard_map/ppermute | solution.py:34
  67.6 9.9 %collective-permute-start.21 = (f32[1,8,128]{2,1,0:T(8,128)S(1)}, f32[1,8,128]{2,1,0:T(8,128)S(1)}, u32[]{:S(2)}, u32[]{:S(2)}) collective-permute-start(f32[1,8,128]{2,1,0:T(8,128)S(1)} %get-tuple-element.226), channel_id=1, source_target_pairs={{4,0},{8,4},{12,8},{5,1},{9,5},{13,9},{6,2},{10,6},{14,10},{7,3},{... | collective-permute-start | bytes 12296 | tf_op jit(solution)/shard_map/ppermute | solution.py:35
  71.9 11.5 %collective-permute-start.16 = (f32[1,16,256]{2,1,0:T(8,128)S(1)}, f32[1,16,256]{2,1,0:T(8,128)S(1)}, u32[]{:S(2)}, u32[]{:S(2)}) collective-permute-start(f32[1,16,256]{2,1,0:T(8,128)S(1)} %get-tuple-element.113), channel_id=1, source_target_pairs={{0,4},{4,8},{8,12},{1,5},{5,9},{9,13},{2,6},{6,10},{10,14},{3,7},{... | collective-permute-start | bytes 49160 | tf_op jit(solution)/shard_map/ppermute | solution.py:34
  73.8 9.6 %collective-permute-start.17 = (f32[1,16,256]{2,1,0:T(8,128)S(1)}, f32[1,16,256]{2,1,0:T(8,128)S(1)}, u32[]{:S(2)}, u32[]{:S(2)}) collective-permute-start(f32[1,16,256]{2,1,0:T(8,128)S(1)} %get-tuple-element.114), channel_id=1, source_target_pairs={{4,0},{8,4},{12,8},{5,1},{9,5},{13,9},{6,2},{10,6},{14,10},{7,3},{... | collective-permute-start | bytes 49160 | tf_op jit(solution)/shard_map/ppermute | solution.py:35
  77.5 29.1 %collective-permute-start.22 = (f32[6,1,128]{2,1,0:T(1,128)S(1)}, f32[6,1,128]{2,1,0:T(1,128)S(1)}, u32[]{:S(2)}, u32[]{:S(2)}) collective-permute-start(f32[6,1,128]{2,1,0:T(1,128)S(1)} %get-tuple-element.190), channel_id=1, source_target_pairs={{0,1},{1,2},{2,3},{4,5},{5,6},{6,7},{8,9},{9,10},{10,11},{12,13},{... | collective-permute-start | bytes 9224 | tf_op jit(solution)/shard_map/ppermute | solution.py:34
  81.0 25.6 %collective-permute-start.23 = (f32[6,1,128]{2,1,0:T(1,128)S(1)}, f32[6,1,128]{2,1,0:T(1,128)S(1)}, u32[]{:S(2)}, u32[]{:S(2)}) collective-permute-start(f32[6,1,128]{2,1,0:T(1,128)S(1)} %get-tuple-element.189), channel_id=1, source_target_pairs={{1,0},{2,1},{3,2},{5,4},{6,5},{7,6},{9,8},{10,9},{11,10},{13,12},{... | collective-permute-start | bytes 9224 | tf_op jit(solution)/shard_map/ppermute | solution.py:35
  83.4 6.0 collective-permute-start.18
  113.6 5.9 collective-permute-start.26
  137.4 33.4 %collective-permute-start.31 = (f32[1,2,4,64]{3,0,2,1:T(1,128)S(1)}, f32[1,2,4,64]{3,0,2,1:T(1,128)S(1)}, u32[]{:S(2)}, u32[]{:S(2)}) collective-permute-start(f32[1,2,4,64]{3,0,2,1:T(1,128)S(1)} %collective-permute-done.30), channel_id=1, source_target_pairs={{0,1},{1,2},{2,3},{3,4},{4,5},{5,6},{6,7},{7,8},{8,9},{9,10},{10,1... | collective-permute-start | bytes 6152 | tf_op jit(solution)/shard_map/ppermute | solution.py:22
  170.8 5.8 collective-permute-start.32
  182.3 5.7 collective-permute-start.34
  188.0 5.7 collective-permute-start.35
  193.8 5.7 collective-permute-start.36
  199.5 5.7 collective-permute-start.37
  205.2 5.7 collective-permute-start.38
  211.0 5.7 collective-permute-start.39
  216.7 5.7 collective-permute-start.40
  222.4 5.7 collective-permute-start.41
  228.2 5.7 collective-permute-start.42
  242.7 7.4 collective-permute-start.45
  244.6 6.7 collective-permute-start.46
  254.0 9.8 %collective-permute-start.47 = (f32[1,16,256]{2,1,0:T(8,128)S(1)}, f32[1,16,256]{2,1,0:T(8,128)S(1)}, u32[]{:S(2)}, u32[]{:S(2)}) collective-permute-start(f32[1,16,256]{2,1,0:T(8,128)S(1)} %get-tuple-element.107), channel_id=1, source_target_pairs={{0,4},{4,8},{8,12},{1,5},{5,9},{9,13},{2,6},{6,10},{10,14},{3,7},{... | collective-permute-start | bytes 49160 | tf_op jit(solution)/shard_map/ppermute | solution.py:34
  255.9 7.9 collective-permute-start.48
  263.9 6.0 collective-permute-start.49
  280.2 6.0 collective-permute-start.53
  309.2 5.9 collective-permute-start.57
  403.9 6.2 collective-permute-start.74
  410.8 7.4 collective-permute-start.76
  412.7 6.7 collective-permute-start.77
  429.1 6.0 collective-permute-start.80
  444.8 6.1 collective-permute-start.84
  527.5 6.0 collective-permute-start.88
  543.5 6.0 collective-permute-start.92
  572.6 5.9 collective-permute-start.96
  674.2 7.4 collective-permute-start.115
  676.1 6.7 collective-permute-start.116
  692.5 6.0 collective-permute-start.119
  708.5 6.2 collective-permute-start.123
  737.6 5.9 collective-permute-start.127
  757.7 5.7 collective-permute-start.131
  763.5 5.7 collective-permute-start.132
  769.2 5.7 collective-permute-start.133
  774.9 5.7 collective-permute-start.134
  780.7 5.7 collective-permute-start.135
  842.0 7.4 collective-permute-start.146
  843.9 6.7 collective-permute-start.147
  861.1 6.0 collective-permute-start.150
  877.4 6.0 collective-permute-start.154
  (141 other events, 3062.9 us)
